TPU v7x, 32 devices: a whole 2x2x4 slice. The times are simulated.
32 devices in a mesh: mkt: 8 (over z, x), grp: 4 (over y, core).
Axes of the slice: x: 2, y: 2, z: 4, core: 2. Of those that a mesh axis runs over, the one named last changes fastest.
Arguments:
- mean_utility: float32 [512, 64], P(('mkt', 'grp')), may hold values from -5 to -1
- market_share: float32 [512, 64], P(('mkt', 'grp')), may hold values from 0.001 to 0.02
- product_traits: float32 [512, 64, 5], P(('mkt', 'grp')), may hold values from -1 to 1
- taste_draws: float32 [512, 5, 1024], P(('mkt', 'grp')), may hold values from -4 to 4
- taste_scale: float32 [5], replicated, may hold values from 0.3 to 1
- type_weight: float32 [512, 1024], P(('mkt', 'grp')), may hold values from 0.1 to 1
- market_size: float32 [512], P(('mkt', 'grp')), may hold values from 0.05 to 3
- product_firm: int32 [512, 64], P(('mkt', 'grp')), may hold values from 0 to 511, all different within a row
- firm_order: int32 [512], replicated, may hold values from 0 to 511, each once
- loyalty: float32 [512, 1024], P(('mkt', 'grp')), may hold values from -1 to 1
- firm_share: float32 [512, 1024], replicated, may hold values from 2e-05 to 0.15
Outputs:
- utility_out: float32 [512, 64], P(('mkt', 'grp'))
- loyalty_out: float32 [512, 1024], P(('mkt', 'grp'))
Inputs may be any that keep to these rules, and one draw needn't show every extreme that they name: `product_firm`: in each market the 64 products belong to 64 different firms, and every firm sells in some market. `firm_order`: each firm appears once.
All inputs are finite; a program needn't handle non-finite values.
Results may differ from a plain program's by a relative error of at most 0.0001.
Values sent between devices are 32-bit elements; how exact they have to be, the bound alone decides.
A program may use at most 64 MiB of HBM per device.

v0:
```python
import functools
import math

import jax
import jax.numpy as jnp
from jax import lax
from jax.experimental import pallas as pl
from jax.experimental.pallas import tpu as pltpu
from jax.sharding import PartitionSpec as P

ITERS = 3
LANES = 128
MESH = pl.DeviceIdType.MESH

clip_target = 0.5
norm_eps = 1e-06


def columns(row):
    return jnp.broadcast_to(row, (LANES, LANES)).T


def split_hi_lo(x):
    hi = x.astype(jnp.bfloat16)
    lo = (x - hi.astype(jnp.float32)).astype(jnp.bfloat16)
    return hi, lo


def kernel(
    dims,
    size_ref, scale_ref, draws_ref, weight_ref, traits_ref, firm_ref, mean_ref, share_own_ref,
    loy_ref, order_ref, share_ref,
    mean_out, loy_out,
    draws, mass, info, loy, means, tbl, tq, tmass, tm_own,
    mass_own, info_own, lmat, one_hot, one_hot_t, taste, col, order_col, order_row, share_v, weighted, table_hl, acc,
    sums, sums_in, totals, totals_in, gap, squares, squares_in, old, old_in, last, last_in,
    copy_sem, draws_s, mass_s, info_s, loy_s, mean_s, tq_s, tm_s, sums_s, totals_s, gap_s, old_s, last_s, sq_s,
):
    mkt, grp, rb, groups, n_m, J, K, firms, owned, R = dims
    n = mkt * grp
    rows = n_m * J
    tiles = rows // LANES
    pair = LANES // J
    qr = firms // groups
    half = groups // 2
    a = lax.axis_index("mkt")
    b = lax.axis_index("grp")
    ao, ai = a // rb, a % rb
    q_me = ao * grp + b
    me = a * grp + b
    side = q_me // half

    barrier = pltpu.get_barrier_semaphore()

    @pl.loop(1, n)
    def _(d):
        t = (me + d) % n
        pl.semaphore_signal(barrier, inc=1, device_id=(t // grp, t % grp), device_id_type=MESH)

    def type_peer(d):
        p = (ai + d) % rb
        return p, (ao * rb + p, b)

    def market_device(q):
        return ((q // grp) * rb + ai, q % grp)

    def market_peer(d):
        q = (q_me + d) % groups
        return q, market_device(q)

    pending = []

    def send(src, dst, sems, mine, theirs, device):
        copy = pltpu.make_async_remote_copy(
            src_ref=src, dst_ref=dst.at[mine], send_sem=sems.at[0, theirs], recv_sem=sems.at[1, mine],
            device_id=device, device_id_type=MESH,
        )
        copy.start()
        pending.append(copy)

    def arrive(dst, sems, theirs, device):
        pltpu.make_async_remote_copy(
            src_ref=dst.at[theirs], dst_ref=dst.at[theirs], send_sem=sems.at[0, theirs], recv_sem=sems.at[1, theirs],
            device_id=device, device_id_type=MESH,
        ).wait_recv()

    def lanes_of(p):
        return pl.ds(pl.multiple_of(p * LANES, LANES), LANES)

    def pack(x):
        return jnp.concatenate([x[i * tiles:(i + 1) * tiles, :] for i in range(pair)], axis=1)

    share_copy = pltpu.make_async_copy(share_ref.at[:, lanes_of(ai)], share_v, copy_sem)
    share_copy.start()

    for k in range(K):
        info_own[k] = pack(traits_ref[k] * scale_ref[k])
    info_own[K] = pack(firm_ref[...].astype(jnp.float32))
    info_own[K + 1] = pack(mean_ref[...])
    for m in range(n_m):
        mass_own[m:m + 1, :] = weight_ref[m:m + 1, :] * size_ref[m]
    info[ai] = info_own[...]

    pl.semaphore_wait(barrier, n - 1)

    for d in range(1, rb):
        p, device = type_peer(d)
        send(loy_ref.at[:, lanes_of(p)], loy, loy_s, ai, p, device)
    for d in range(1, rb):
        p, device = type_peer(d)
        send(info_own, info, info_s, ai, p, device)
        send(draws_ref.at[:, lanes_of(p)], draws, draws_s, ai, p, device)
        send(mass_own.at[:, lanes_of(p)], mass, mass_s, ai, p, device)

    draws[ai] = draws_ref[:, lanes_of(ai)]
    mass[ai] = mass_own[:, lanes_of(ai)]
    loy[ai] = loy_ref[:, lanes_of(ai)]

    for i in range(firms // LANES):
        col[i * LANES:(i + 1) * LANES, :] = columns(order_ref[i:i + 1, :].astype(jnp.float32))
    for q in range(groups):
        for p in range(rb):
            src = (((q // grp) * rb + p) * grp + q % grp) * owned
            dst = (q * rb + p) * owned
            order_col[dst:dst + owned, :] = col[src:src + owned, :]
    for i in range(firms // LANES):
        order_row[0:1, i * LANES:(i + 1) * LANES] = order_col[i * LANES:(i + 1) * LANES, :].T[0:1, :]

    for d in range(1, rb):
        p, device = type_peer(d)
        arrive(loy, loy_s, p, device)
    for p in range(rb):
        tq[p * owned:(p + 1) * owned, :] = loy[p]
    for d in range(1, groups):
        q, device = market_peer(d)
        send(tq, tbl, tq_s, q_me, q, device)
    tbl[q_me] = tq[...]

    row = lax.broadcasted_iota(jnp.int32, (n_m * K, LANES), 0)
    lane = lax.broadcasted_iota(jnp.int32, (n_m * K, LANES), 1)
    trait_of = row // n_m
    offset = row % n_m - (lane // J) * tiles

    def prepare(p):
        for i in range(tiles):
            traits = jnp.zeros((n_m * K, LANES), jnp.float32)
            for k in range(K):
                traits = jnp.where(trait_of == k, info[p, k, i:i + 1, :], traits)
            lmat[:, i * LANES:(i + 1) * LANES] = jnp.where(offset == i, traits, 0.0)
        taste[p] = lax.dot_general(
            lmat[...], draws[p], (((0,), (0,)), ((), ())),
            precision=lax.Precision.HIGHEST, preferred_element_type=jnp.float32,
        )
        for i in range(tiles):
            firm_row = info[p, K, i:i + 1, :]
            firm_col = columns(firm_row)
            for f in range(firms // LANES):
                one_hot[p, i * LANES:(i + 1) * LANES, f * LANES:(f + 1) * LANES] = (
                    firm_col == order_row[0:1, f * LANES:(f + 1) * LANES]
                ).astype(jnp.float32).astype(jnp.bfloat16)
            one_hot_t[p, :, i * LANES:(i + 1) * LANES] = (
                order_col[...] == firm_row
            ).astype(jnp.float32).astype(jnp.bfloat16)

    prepare(ai)

    share_copy.wait()
    first = pl.multiple_of(q_me * qr, 8)
    mine_col = order_col[pl.ds(first, qr), :]
    number = lax.broadcasted_iota(jnp.int32, (qr, LANES), 1).astype(jnp.float32)
    my_share = jnp.zeros((qr, LANES), jnp.float32)
    for i in range(firms // LANES):
        pick = (mine_col == number + float(i * LANES)).astype(jnp.float32)
        my_share += jnp.dot(
            pick, share_v[i * LANES:(i + 1) * LANES, :],
            precision=lax.Precision.HIGHEST, preferred_element_type=jnp.float32,
        )
    my_share = jnp.log(my_share)

    share_own = share_own_ref[...]
    base = jnp.log(share_own) + jnp.log(jnp.sum(mass_own[...], axis=1, keepdims=True))
    base = pack(base)

    for d in range(1, groups):
        q, device = market_peer(d)
        arrive(tbl, tq_s, q, device)

    def split_table():
        for q in range(groups):
            hi, lo = split_hi_lo(tbl[q])
            table_hl[q * qr:(q + 1) * qr, :LANES] = hi
            table_hl[q * qr:(q + 1) * qr, LANES:] = lo

    per_block = 2
    block = per_block * LANES

    def shares(it, p):
        mean_rows = info[p, K + 1] if it == 0 else means[it - 1, p]
        for h in range(rows // block):
            r0 = h * block
            both = jnp.dot(
                one_hot[p, r0:r0 + block, :], table_hl[...], preferred_element_type=jnp.float32
            )
            mean_col = jnp.concatenate(
                [columns(mean_rows[i:i + 1, :]) for i in range(h * per_block, (h + 1) * per_block)], axis=0
            )
            expu = jnp.exp(both[:, :LANES] + both[:, LANES:] + mean_col + taste[p, r0:r0 + block, :])
            parts = []
            for i in range(per_block):
                for s in range(pair):
                    part = expu[i * LANES + s * J:i * LANES + (s + 1) * J, :]
                    m = s * tiles + h * per_block + i
                    parts.append(
                        part * (mass[p, m:m + 1, :] / (1.0 + jnp.sum(part, axis=0, keepdims=True)))
                    )
            bought = jnp.concatenate(parts, axis=0)
            for i in range(per_block):
                at = h * per_block + i
                sums[it, p, at:at + 1, :] = jnp.sum(
                    bought[i * LANES:(i + 1) * LANES, :].T, axis=0, keepdims=True
                )
            hi, lo = split_hi_lo(bought)
            weighted[p, r0:r0 + block, :LANES] = hi
            weighted[p, r0:r0 + block, LANES:] = lo

    def half_totals(it, which):
        begin = pl.multiple_of(which * (half * qr), 16)
        acc[...] = jnp.zeros_like(acc)

        @pl.loop(0, rb)
        def _(p):
            acc[...] += jnp.dot(
                one_hot_t[p, pl.ds(begin, half * qr), :], weighted[p], preferred_element_type=jnp.float32
            )

        for j in range(half):
            totals[it, which * half + j] = (
                acc[j * qr:(j + 1) * qr, :LANES] + acc[j * qr:(j + 1) * qr, LANES:]
            )

    mean_now = pack(mean_ref[...])
    log_mass = None
    for it in range(ITERS):
        final = it == ITERS - 1
        if final:
            mine = tbl[q_me]
            for p in range(rb):
                old[p] = mine[p * owned:(p + 1) * owned, :]
            for d in range(1, rb):
                p, device = type_peer(d)
                send(old.at[p], old_in, old_s, ai, p, device)
            old_in[ai] = old[ai]
        split_table()
        if it == 0:
            shares(0, ai)

            @pl.loop(1, rb)
            def _(d):
                p, device = type_peer(d)
                arrive(info, info_s, p, device)
                arrive(draws, draws_s, p, device)
                arrive(mass, mass_s, p, device)
                prepare(p)
                shares(0, p)

            tm_own[...] = jnp.zeros_like(tm_own)
            for p in range(rb):
                tm_own[...] += jnp.sum(mass[p], axis=0, keepdims=True)
            for d in range(1, groups):
                q, device = market_peer(d)
                send(tm_own, tmass, tm_s, q_me, q, device)
            tmass[q_me] = tm_own[...]
        else:
            @pl.loop(0, rb)
            def _(p):
                shares(it, p)

        for d in range(1, rb):
            p, device = type_peer(d)
            send(sums.at[it, p], sums_in.at[it], sums_s.at[it], ai, p, device)
        sums_in[it, ai] = sums[it, ai]

        half_totals(it, 1 - side)
        for j in range(half):
            q = (1 - side) * half + (q_me + j) % half
            send(totals.at[it, q], totals_in.at[it], totals_s.at[it], q_me, q, market_device(q))
        half_totals(it, side)
        for j in range(1, half):
            q = side * half + (q_me + j) % half
            send(totals.at[it, q], totals_in.at[it], totals_s.at[it], q_me, q, market_device(q))
        totals_in[it, q_me] = totals[it, q_me]

        for d in range(1, rb):
            p, device = type_peer(d)
            arrive(sums_in.at[it], sums_s.at[it], p, device)
        mean_now = mean_now + base - jnp.log(jnp.sum(sums_in[it], axis=0))
        if final:
            for i in range(pair):
                mean_out[i * tiles:(i + 1) * tiles, :] = mean_now[:, i * J:(i + 1) * J]
        else:
            means[it, ai] = mean_now
            for d in range(1, rb):
                p, device = type_peer(d)
                send(means.at[it, ai], means.at[it], mean_s.at[it], ai, p, device)

        if it == 0:
            for d in range(1, groups):
                q, device = market_peer(d)
                arrive(tmass, tm_s, q, device)
            log_mass = jnp.log(jnp.sum(tmass[...], axis=0))
        for d in range(1, groups):
            q, device = market_peer(d)
            arrive(totals_in.at[it], totals_s.at[it], q, device)
        gap_mine = my_share - (jnp.log(jnp.sum(totals_in[it], axis=0)) - log_mass)
        squares[it] = jnp.sum(gap_mine * gap_mine, axis=0, keepdims=True)

        @pl.loop(1, n)
        def _(d):
            t = (me + d) % n
            pltpu.make_async_remote_copy(
                src_ref=squares.at[it], dst_ref=squares_in.at[it, d - 1],
                send_sem=sq_s.at[0, it], recv_sem=sq_s.at[1, it],
                device_id=(t // grp, t % grp), device_id_type=MESH,
            ).start()

        if final:
            for p in range(rb):
                last[p] = gap_mine[p * owned:(p + 1) * owned, :]
            for d in range(1, rb):
                p, device = type_peer(d)
                send(last.at[p], last_in, last_s, ai, p, device)
            last_in[ai] = last[ai]
        else:
            gap[it, q_me] = gap_mine
            for d in range(1, groups):
                q, device = market_peer(d)
                send(gap.at[it, q_me], gap.at[it], gap_s.at[it], q_me, q, device)

        pltpu.make_async_copy(squares_in.at[it], squares_in.at[it], sq_s.at[1, it]).wait()
        total = jnp.sum(jnp.sum(squares_in[it], axis=0) + squares[it], axis=1, keepdims=True)
        clip = jnp.minimum(1.0, clip_target / jnp.sqrt(total / (firms * R) + norm_eps))

        if final:
            for d in range(1, rb):
                p, device = type_peer(d)
                arrive(old_in, old_s, p, device)
                arrive(last_in, last_s, p, device)
            for p in range(rb):
                loy_out[:, p * LANES:(p + 1) * LANES] = old_in[p] + clip * last_in[p]
        else:
            for d in range(1, groups):
                q, device = market_peer(d)
                arrive(gap.at[it], gap_s.at[it], q, device)
            for q in range(groups):
                tbl[q] = tbl[q] + clip * gap[it, q]
            for d in range(1, rb):
                p, device = type_peer(d)
                arrive(means.at[it], mean_s.at[it], p, device)

    for it in range(ITERS):
        pltpu.make_async_copy(squares_in.at[it], squares_in.at[it], sq_s.at[0, it]).wait()
    for copy in pending:
        copy.wait_send()


def local(
    mkt, grp,
    mean_utility, market_share, product_traits, taste_draws, taste_scale, type_weight,
    market_size, product_firm, firm_order, loyalty, firm_share,
):
    n_m, J, K = product_traits.shape
    firms, R = firm_share.shape
    owned = loyalty.shape[0]
    rb = R // LANES
    groups = mkt * grp // rb
    rows = n_m * J
    tiles = rows // LANES
    qr = firms // groups

    f32, bf16 = jnp.float32, jnp.bfloat16
    dma = pltpu.SemaphoreType.DMA
    vmem = pltpu.VMEM
    spec = pl.BlockSpec(memory_space=pltpu.VMEM)
    smem = pl.BlockSpec(memory_space=pltpu.SMEM)
    dims = (mkt, grp, rb, groups, n_m, J, K, firms, owned, R)
    scratch = [
        vmem((rb, n_m * K, LANES), f32),
        vmem((rb, n_m, LANES), f32),
        vmem((rb, K + 2, tiles, LANES), f32),
        vmem((rb, owned, LANES), f32),
        vmem((ITERS - 1, rb, tiles, LANES), f32),
        vmem((groups, qr, LANES), f32),
        vmem((qr, LANES), f32),
        vmem((groups, 1, LANES), f32),
        vmem((1, LANES), f32),
        vmem((n_m, R), f32),
        vmem((K + 2, tiles, LANES), f32),
        vmem((n_m * K, rows), f32),
        vmem((rb, rows, firms), bf16),
        vmem((rb, firms, rows), bf16),
        vmem((rb, rows, LANES), f32),
        vmem((firms, LANES), f32),
        vmem((firms, LANES), f32),
        vmem((1, firms), f32),
        vmem((firms, LANES), f32),
        vmem((rb, rows, 2 * LANES), bf16),
        vmem((firms, 2 * LANES), bf16),
        vmem((firms // 2, 2 * LANES), f32),
        vmem((ITERS, rb, tiles, LANES), f32),
        vmem((ITERS, rb, tiles, LANES), f32),
        vmem((ITERS, groups, qr, LANES), f32),
        vmem((ITERS, groups, qr, LANES), f32),
        vmem((ITERS - 1, groups, qr, LANES), f32),
        vmem((ITERS, 1, LANES), f32),
        vmem((ITERS, mkt * grp - 1, 1, LANES), f32),
        vmem((rb, owned, LANES), f32),
        vmem((rb, owned, LANES), f32),
        vmem((rb, owned, LANES), f32),
        vmem((rb, owned, LANES), f32),
        dma,
        dma((2, rb)), dma((2, rb)), dma((2, rb)), dma((2, rb)),
        dma((ITERS - 1, 2, rb)),
        dma((2, groups)), dma((2, groups)),
        dma((ITERS, 2, rb)),
        dma((ITERS, 2, groups)),
        dma((ITERS - 1, 2, groups)),
        dma((2, rb)), dma((2, rb)),
        dma((2, ITERS)),
    ]
    return pl.pallas_call(
        functools.partial(kernel, dims),
        out_shape=(
            jax.ShapeDtypeStruct((n_m, J), f32),
            jax.ShapeDtypeStruct((owned, R), f32),
        ),
        in_specs=[smem] * 2 + [spec] * 8 + [pl.BlockSpec(memory_space=pl.ANY)],
        out_specs=(spec, spec),
        scratch_shapes=scratch,
        compiler_params=pltpu.CompilerParams(
            collective_id=0, has_side_effects=True, vmem_limit_bytes=60 * 1024 * 1024
        ),
    )(
        market_size, taste_scale, taste_draws.transpose(1, 0, 2).reshape(n_m * K, R), type_weight,
        product_traits.transpose(2, 0, 1), product_firm, mean_utility, market_share,
        loyalty, firm_order.reshape(firms // LANES, LANES), firm_share,
    )


def solution(mesh):
    both = ("mkt", "grp")
    placed = (
        P(both, None), P(both, None), P(both, None, None), P(both, None, None), P(),
        P(both, None), P(both), P(both, None), P(), P(both, None), P(),
    )
    return jax.shard_map(
        functools.partial(local, mesh.shape["mkt"], mesh.shape["grp"]),
        mesh=mesh,
        in_specs=placed,
        out_specs=(P(both, None), P(both, None)),
        check_vma=False,
    )
```

profile of v0, /device:TPU:0, one launch (start us, length us, event | category | flops | bytes accessed | tf_op | source)
XLA Modules:
  0.0 87.9 jit_solution(10694471133246648394)
XLA Ops:
  0.6 84.5 %shard_map.122 = (f32[16,64]{1,0:T(8,128)}, f32[16,1024]{1,0:T(8,128)}) custom-call(f32[16]{0:T(128)} %size_ref.1, f32[5]{0:T(128)} %scale_ref.1, f32[80,1024]{1,0:T(8,128)} %bitcast.5, f32[16,1024]{1,0:T(8,128)} %weight_ref.1, f32[5,16,64]{2,1,0:T(8,128)} %bitcast.6, s32[16,64]{1,0:T(8,128)} %firm_ref.1, f32[16,64]{1,0:T(8,128)} %mean_ref.1, ...), custom_call_target="tpu_custom_call" | custom-call | tf_op jit(solution)/shard_map/pallas_call | solution.py:430
  85.1 1.3 %copy.15 = f32[16,64]{1,0:T(8,128)} copy(f32[16,64]{1,0:T(8,128)} %get-tuple-element.4) | data formatting | bytes 8192
  86.4 1.5 %copy.16 = f32[16,1024]{1,0:T(8,128)} copy(f32[16,1024]{1,0:T(8,128)} %get-tuple-element.5) | data formatting | bytes 131072
where the time goes:
time: 88.1 us; the launch traced here: 87.9 us
  Pallas kernels  84.5 us (96%)
  local copies, waits for them, and re-layouts  2.77 us (3%)
    pallas_call x1, Pallas kernels, local(): pl.pallas_call(functools.partial(kernel, dims), out_shape=(jax.ShapeDtype...  84.5 us
    unnamed x2, local copies, waits for them, and re-layouts  2.77 us

commit v1 on v0

v1 whole, which is shorter than its diff:
```python
import functools

import jax
import jax.numpy as jnp
from jax import lax
from jax.experimental import pallas as pl
from jax.experimental.pallas import tpu as pltpu
from jax.sharding import PartitionSpec as P

ITERS = 3
LANES = 128
MESH = pl.DeviceIdType.MESH

clip_target = 0.5
norm_eps = 1e-06

scope = jax.named_scope


def columns(row):
    return jnp.broadcast_to(row, (LANES, LANES)).T


def split_hi_lo(x):
    hi = x.astype(jnp.bfloat16)
    lo = (x - hi.astype(jnp.float32)).astype(jnp.bfloat16)
    return hi, lo


def xor(x, d, size):
    out = x
    bit = 1
    while bit < size:
        out = out + ((d // bit) % 2) * (1 - 2 * ((x // bit) % 2)) * bit
        bit *= 2
    return out


def kernel(
    dims,
    size_h, scale_h, draws_h, weight_h, traits_h, firm_h, mean_h, share_own_h, loy_h, order_h, share_h,
    mean_out, loy_out,
    size_ref, scale_ref, weight_ref, traits_ref, firm_ref, mean_ref, share_own_ref, order_ref, share_v,
    draws, mass, info, loy, means, tbl, tq, tmass, tm_own,
    mass_own, lmat, rmat, one_hot, util, near_gap, col, order_col, order_row, table_hl, weighted,
    sums, sums_in, totals, totals_in, gap, squares, squares_in, old, old_in, last, last_in,
    in_s, draws_s, mass_s, info_s, loy_s, mean_s, tq_s, tm_s, sums_s, totals_s, gap_s, old_s, last_s, sq_s,
):
    mkt, grp, rb, groups, n_m, J, K, firms, owned, R = dims
    n = mkt * grp
    rows = n_m * J
    tiles = rows // LANES
    pair = LANES // J
    qr = firms // groups
    half = groups // 2
    near = half * qr
    a = lax.axis_index("mkt")
    b = lax.axis_index("grp")
    ao, ai = a // rb, a % rb
    q_me = ao * grp + b
    me = a * grp + b

    def type_lane(d):
        return xor(ai, d, rb)

    def type_device(d):
        return (ao * rb + xor(ai, d, rb), b)

    def market_device(j):
        q = xor(q_me, j, groups)
        return ((q // grp) * rb + ai, q % grp)

    def lanes_of(p):
        return pl.ds(pl.multiple_of(p * LANES, LANES), LANES)

    pending = []

    def send(src, dst, sems, slot, device):
        copy = pltpu.make_async_remote_copy(
            src_ref=src, dst_ref=dst, send_sem=sems.at[0, slot], recv_sem=sems.at[1, slot],
            device_id=device, device_id_type=MESH,
        )
        copy.start()
        pending.append(copy)

    def arrive(dst, sems, slot):
        pltpu.make_async_copy(dst, dst, sems.at[1, slot]).wait()

    def pack(x):
        return jnp.concatenate([x[i * tiles:(i + 1) * tiles, :] for i in range(pair)], axis=1)

    inputs = {}
    for at, (key, src, dst) in enumerate((
        ("weight", weight_h, weight_ref), ("traits", traits_h, traits_ref), ("firm", firm_h, firm_ref),
        ("mean", mean_h, mean_ref), ("size", size_h, size_ref), ("scale", scale_h, scale_ref),
        ("draws", draws_h.at[:, lanes_of(ai)], draws.at[0]), ("loy", loy_h.at[:, lanes_of(ai)], loy.at[0]),
        ("order", order_h, order_ref), ("share_own", share_own_h, share_own_ref),
        ("share", share_h.at[:, lanes_of(ai)], share_v),
    )):
        inputs[key] = pltpu.make_async_copy(src, dst, in_s.at[at])
        inputs[key].start()

    barrier = pltpu.get_barrier_semaphore()

    @pl.loop(1, n)
    def _(d):
        t = (me + d) % n
        pl.semaphore_signal(barrier, inc=1, device_id=(t // grp, t % grp), device_id_type=MESH)

    for key in ("weight", "traits", "firm", "mean", "size", "scale"):
        inputs[key].wait()
    for k in range(K):
        info[0, k] = pack(traits_ref[k] * scale_ref[k])
    info[0, K] = pack(firm_ref[...].astype(jnp.float32))
    mean_now = pack(mean_ref[...])
    info[0, K + 1] = mean_now
    for m in range(n_m):
        mass_own[m:m + 1, :] = weight_ref[m:m + 1, :] * size_ref[m]

    with scope("bar"):
        pl.semaphore_wait(barrier, n - 1)

    for d in range(1, rb):
        send(loy_h.at[:, lanes_of(type_lane(d))], loy.at[d], loy_s, d, type_device(d))
    for d in range(1, rb):
        device = type_device(d)
        lanes = lanes_of(type_lane(d))
        send(draws_h.at[:, lanes], draws.at[d], draws_s, d, device)
        send(info.at[0], info.at[d], info_s, d, device)
        send(mass_own.at[:, lanes], mass.at[d], mass_s, d, device)

    mass[0] = mass_own[:, lanes_of(ai)]

    for key in ("order", "draws", "loy"):
        inputs[key].wait()
    for i in range(firms // LANES):
        col[i * LANES:(i + 1) * LANES, :] = columns(order_ref[i:i + 1, :].astype(jnp.float32))
    for j in range(groups):
        q = xor(q_me, j, groups)
        for d in range(rb):
            src = (((q // grp) * rb + xor(ai, d, rb)) * grp + q % grp) * owned
            dst = (j * rb + d) * owned
            order_col[dst:dst + owned, :] = col[pl.ds(pl.multiple_of(src, owned), owned), :]
    for i in range(firms // LANES):
        order_row[0:1, i * LANES:(i + 1) * LANES] = order_col[i * LANES:(i + 1) * LANES, :].T[0:1, :]

    kk = n_m * K
    row = lax.broadcasted_iota(jnp.int32, (n_m, LANES), 0)
    lane = lax.broadcasted_iota(jnp.int32, (n_m, LANES), 1)
    offset = row - (lane // J) * tiles
    zero = jnp.zeros((n_m, LANES), jnp.float32)
    rmat[kk:, :] = jnp.zeros_like(rmat[kk:, :])
    rmat[2 * kk:, :LANES] = jnp.ones_like(rmat[2 * kk:, :LANES])

    def rows_of(d, r0, count):
        return pl.ds(pl.multiple_of(d * rows + r0, LANES), count)

    def spread(part, where):
        return jnp.where(where, jnp.broadcast_to(part.astype(jnp.float32), (n_m, LANES)), zero).astype(jnp.bfloat16)

    def prepare(d):
        hi, lo = split_hi_lo(draws[d])
        rmat[:kk, :LANES] = hi
        rmat[:kk, LANES:] = lo
        rmat[kk:2 * kk, :LANES] = hi
        for i in range(tiles):
            here = offset == i
            at = slice(i * LANES, (i + 1) * LANES)
            for k in range(K):
                hi, lo = split_hi_lo(info[d, k, i:i + 1, :])
                lmat[k * n_m:(k + 1) * n_m, at] = spread(hi, here)
                lmat[kk + k * n_m:kk + (k + 1) * n_m, at] = spread(lo, here)
            rest = info[d, K + 1, i:i + 1, :]
            for s in range(3):
                hi = rest.astype(jnp.bfloat16)
                rest = rest - hi.astype(jnp.float32)
                lmat[2 * kk + s * n_m:2 * kk + (s + 1) * n_m, at] = spread(hi, here)
        both = lax.dot_general(
            lmat[...], rmat[...], (((0,), (0,)), ((), ())), preferred_element_type=jnp.float32
        )
        util[rows_of(d, 0, rows), :] = both[:, :LANES] + both[:, LANES:]
        for i in range(tiles):
            firm_col = columns(info[d, K, i:i + 1, :])
            for f in range(firms // LANES):
                one_hot[rows_of(d, i * LANES, LANES), f * LANES:(f + 1) * LANES] = (
                    firm_col == order_row[0:1, f * LANES:(f + 1) * LANES]
                ).astype(jnp.float32).astype(jnp.bfloat16)

    with scope("prep0"):
        prepare(0)

    with scope("arr_loy"):
        for d in range(1, rb):
            arrive(loy.at[d], loy_s, d)
    for d in range(rb):
        tq[d * owned:(d + 1) * owned, :] = loy[d]
    for j in range(1, groups):
        send(tq, tbl.at[j], tq_s, j, market_device(j))
    tbl[0] = tq[...]

    def arrive_inputs(d):
        arrive(info.at[d], info_s, d)
        arrive(draws.at[d], draws_s, d)
        arrive(mass.at[d], mass_s, d)

    first = rb // 2

    @pl.loop(1, first)
    def _(d):
        with scope("arr_a"):
            arrive_inputs(d)
        with scope("prep_a"):
            prepare(d)

    with scope("share"):
        inputs["share"].wait()
        inputs["share_own"].wait()
        mine_col = order_col[:qr, :]
        number = lax.broadcasted_iota(jnp.int32, (qr, LANES), 1).astype(jnp.float32)
        my_share = jnp.zeros((qr, LANES), jnp.float32)
        for i in range(firms // LANES):
            pick = (mine_col == number + float(i * LANES)).astype(jnp.float32)
            my_share += jnp.dot(
                pick, share_v[i * LANES:(i + 1) * LANES, :],
                precision=lax.Precision.HIGHEST, preferred_element_type=jnp.float32,
            )
        my_share = jnp.log(my_share)
        base = jnp.log(share_own_ref[...]) + jnp.log(jnp.sum(mass_own[...], axis=1, keepdims=True))
        base = pack(base)

    with scope("arr_tbl"):
        for j in range(1, groups):
            arrive(tbl.at[j], tq_s, j)

    def split_into(j, value):
        hi, lo = split_hi_lo(value)
        table_hl[j * qr:(j + 1) * qr, :LANES] = hi
        table_hl[j * qr:(j + 1) * qr, LANES:] = lo

    for j in range(groups):
        split_into(j, tbl[j])

    per_block = 2
    block = per_block * LANES

    def gather(d, r0, begin, end):
        both = jnp.dot(
            one_hot[rows_of(d, r0, block), begin:end], table_hl[begin:end, :], preferred_element_type=jnp.float32
        )
        return both[:, :LANES] + both[:, LANES:]

    def shares(it, d, clip):
        for h in range(rows // block):
            r0 = h * block
            at = rows_of(d, r0, block)
            if it == 0:
                u = util[at, :] + gather(d, r0, 0, firms)
            else:
                u = util[at, :] + clip * (near_gap[at, :] + gather(d, r0, near, firms))
            if it < ITERS - 1:
                util[at, :] = u
            expu = jnp.exp(u)
            for i in range(per_block):
                t = h * per_block + i
                parts = []
                for s in range(pair):
                    part = expu[i * LANES + s * J:i * LANES + (s + 1) * J, :]
                    m = s * tiles + t
                    parts.append(
                        part * (mass[d, m:m + 1, :] / (1.0 + jnp.sum(part, axis=0, keepdims=True)))
                    )
                bought = jnp.concatenate(parts, axis=0).T
                sums[it, d, t:t + 1, :] = jnp.sum(bought, axis=0, keepdims=True)
                hi, lo = split_hi_lo(bought)
                lanes = rows_of(d, t * LANES, LANES)
                weighted[:LANES, lanes] = hi
                weighted[LANES:, lanes] = lo

    def half_totals(it, begin):
        acc = jnp.dot(
            weighted[...], one_hot[:, begin * qr:(begin + half) * qr], preferred_element_type=jnp.float32
        )
        acc = acc[:LANES, :] + acc[LANES:, :]
        acc = jnp.concatenate([acc[:, i * LANES:(i + 1) * LANES].T for i in range(near // LANES)], axis=0)
        for j in range(half):
            totals[it, begin + j] = acc[j * qr:(j + 1) * qr, :]

    clip = None
    log_mass = None
    for it in range(ITERS):
        final = it == ITERS - 1
        if it == 0:
            with scope("sh_a"):
                @pl.loop(0, first)
                def _(d):
                    shares(0, d, None)

            @pl.loop(first, rb)
            def _(d):
                with scope("arr_b"):
                    arrive_inputs(d)
                with scope("prep_b"):
                    prepare(d)
                with scope("sh_b"):
                    shares(0, d, None)

            tm_own[...] = jnp.zeros_like(tm_own)
            for d in range(rb):
                tm_own[...] += jnp.sum(mass[d], axis=0, keepdims=True)
            for j in range(1, groups):
                send(tm_own, tmass.at[j], tm_s, j, market_device(j))
            tmass[0] = tm_own[...]
        else:
            with scope("shares%d" % it):
                @pl.loop(0, rb)
                def _(d):
                    shares(it, d, clip)

        for d in range(1, rb):
            send(sums.at[it, d], sums_in.at[it, d], sums_s.at[it], d, type_device(d))
        sums_in[it, 0] = sums[it, 0]

        with scope("far%d" % it):
            half_totals(it, half)
        for j in range(half, groups):
            send(totals.at[it, j], totals_in.at[it, j], totals_s.at[it], j, market_device(j))
        with scope("near%d" % it):
            half_totals(it, 0)
        for j in range(1, half):
            send(totals.at[it, j], totals_in.at[it, j], totals_s.at[it], j, market_device(j))
        totals_in[it, 0] = totals[it, 0]

        if final:
            for d in range(rb):
                old[d] = tbl[0, d * owned:(d + 1) * owned, :]
            for d in range(1, rb):
                send(old.at[d], old_in.at[d], old_s, d, type_device(d))
            old_in[0] = old[0]

        if it == 0:
            for j in range(1, groups):
                arrive(tmass.at[j], tm_s, j)
            log_mass = jnp.log(jnp.sum(tmass[...], axis=0))

        with scope("arr_sums%d" % it):
            for d in range(1, rb):
                arrive(sums_in.at[it, d], sums_s.at[it], d)
        step = base - jnp.log(jnp.sum(sums_in[it], axis=0))
        mean_now = mean_now + step
        if final:
            for i in range(pair):
                mean_out[i * tiles:(i + 1) * tiles, :] = mean_now[:, i * J:(i + 1) * J]
        else:
            means[it, 0] = step
            for d in range(1, rb):
                send(means.at[it, 0], means.at[it, d], mean_s.at[it], d, type_device(d))

        with scope("arr_tot%d" % it):
            for j in range(1, groups):
                arrive(totals_in.at[it, j], totals_s.at[it], j)
        gap_mine = my_share - (jnp.log(jnp.sum(totals_in[it], axis=0)) - log_mass)
        squares[it] = jnp.sum(gap_mine * gap_mine, axis=0, keepdims=True)

        @pl.loop(1, n)
        def _(d):
            t = (me + d) % n
            pltpu.make_async_remote_copy(
                src_ref=squares.at[it], dst_ref=squares_in.at[it, d - 1],
                send_sem=sq_s.at[0, it], recv_sem=sq_s.at[1, it],
                device_id=(t // grp, t % grp), device_id_type=MESH,
            ).start()

        if final:
            for d in range(rb):
                last[d] = gap_mine[d * owned:(d + 1) * owned, :]
            for d in range(1, rb):
                send(last.at[d], last_in.at[d], last_s, d, type_device(d))
            last_in[0] = last[0]
        else:
            gap[it, 0] = gap_mine
            for j in [*range(half, groups), *range(1, half)]:
                send(gap.at[it, 0], gap.at[it, j], gap_s.at[it], j, market_device(j))
            for j in range(half):
                if j:
                    arrive(gap.at[it, j], gap_s.at[it], j)
                split_into(j, gap[it, j])

            with scope("gnear%d" % it):
                @pl.loop(0, rb)
                def _(d):
                    for r0 in range(0, rows, block):
                        near_gap[rows_of(d, r0, block), :] = gather(d, r0, 0, near)

            with scope("arr_mean%d" % it):
                for d in range(1, rb):
                    arrive(means.at[it, d], mean_s.at[it], d)

            with scope("addmean%d" % it):
                @pl.loop(0, rb)
                def _(d):
                    for i in range(tiles):
                        at = rows_of(d, i * LANES, LANES)
                        util[at, :] = util[at, :] + columns(means[it, d, i:i + 1, :])

            with scope("arr_gap%d" % it):
                for j in range(half, groups):
                    arrive(gap.at[it, j], gap_s.at[it], j)
                    split_into(j, gap[it, j])

        with scope("arr_sq%d" % it):
            pltpu.make_async_copy(squares_in.at[it], squares_in.at[it], sq_s.at[1, it]).wait()
        total = jnp.sum(jnp.sum(squares_in[it], axis=0) + squares[it], axis=1, keepdims=True)
        clip = jnp.minimum(1.0, clip_target / jnp.sqrt(total / (firms * R) + norm_eps))

        if final:
            with scope("arr_last"):
                for d in range(1, rb):
                    arrive(old_in.at[d], old_s, d)
                    arrive(last_in.at[d], last_s, d)
            for d in range(rb):
                loy_out[:, lanes_of(type_lane(d))] = old_in[d] + clip * last_in[d]
        else:
            tbl[0] = tbl[0] + clip * gap_mine

    with scope("drain"):
        for it in range(ITERS):
            pltpu.make_async_copy(squares_in.at[it], squares_in.at[it], sq_s.at[0, it]).wait()
        for copy in pending:
            copy.wait_send()


def local(
    mkt, grp,
    mean_utility, market_share, product_traits, taste_draws, taste_scale, type_weight,
    market_size, product_firm, firm_order, loyalty, firm_share,
):
    n_m, J, K = product_traits.shape
    firms, R = firm_share.shape
    owned = loyalty.shape[0]
    rb = R // LANES
    groups = mkt * grp // rb
    rows = n_m * J
    tiles = rows // LANES
    qr = firms // groups
    depth = n_m * (2 * K + 3)

    f32, bf16 = jnp.float32, jnp.bfloat16
    dma = pltpu.SemaphoreType.DMA
    vmem = pltpu.VMEM
    spec = pl.BlockSpec(memory_space=pltpu.VMEM)
    dims = (mkt, grp, rb, groups, n_m, J, K, firms, owned, R)
    scratch = [
        pltpu.SMEM((n_m,), f32),
        pltpu.SMEM((K,), f32),
        vmem((n_m, R), f32),
        vmem((K, n_m, J), f32),
        vmem((n_m, J), jnp.int32),
        vmem((n_m, J), f32),
        vmem((n_m, J), f32),
        vmem((firms // LANES, LANES), jnp.int32),
        vmem((firms, LANES), f32),
        vmem((rb, n_m * K, LANES), f32),
        vmem((rb, n_m, LANES), f32),
        vmem((rb, K + 2, tiles, LANES), f32),
        vmem((rb, owned, LANES), f32),
        vmem((ITERS - 1, rb, tiles, LANES), f32),
        vmem((groups, qr, LANES), f32),
        vmem((qr, LANES), f32),
        vmem((groups, 1, LANES), f32),
        vmem((1, LANES), f32),
        vmem((n_m, R), f32),
        vmem((depth, rows), bf16),
        vmem((depth, 2 * LANES), bf16),
        vmem((rb * rows, firms), bf16),
        vmem((rb * rows, LANES), f32),
        vmem((rb * rows, LANES), f32),
        vmem((firms, LANES), f32),
        vmem((firms, LANES), f32),
        vmem((1, firms), f32),
        vmem((firms, 2 * LANES), bf16),
        vmem((2 * LANES, rb * rows), bf16),
        vmem((ITERS, rb, tiles, LANES), f32),
        vmem((ITERS, rb, tiles, LANES), f32),
        vmem((ITERS, groups, qr, LANES), f32),
        vmem((ITERS, groups, qr, LANES), f32),
        vmem((ITERS - 1, groups, qr, LANES), f32),
        vmem((ITERS, 1, LANES), f32),
        vmem((ITERS, mkt * grp - 1, 1, LANES), f32),
        vmem((rb, owned, LANES), f32),
        vmem((rb, owned, LANES), f32),
        vmem((rb, owned, LANES), f32),
        vmem((rb, owned, LANES), f32),
        dma((11,)),
        dma((2, rb)), dma((2, rb)), dma((2, rb)), dma((2, rb)),
        dma((ITERS - 1, 2, rb)),
        dma((2, groups)), dma((2, groups)),
        dma((ITERS, 2, rb)),
        dma((ITERS, 2, groups)),
        dma((ITERS - 1, 2, groups)),
        dma((2, rb)), dma((2, rb)),
        dma((2, ITERS)),
    ]
    return pl.pallas_call(
        functools.partial(kernel, dims),
        out_shape=(
            jax.ShapeDtypeStruct((n_m, J), f32),
            jax.ShapeDtypeStruct((owned, R), f32),
        ),
        in_specs=[pl.BlockSpec(memory_space=pl.ANY)] * 11,
        out_specs=(spec, spec),
        scratch_shapes=scratch,
        compiler_params=pltpu.CompilerParams(
            collective_id=0, has_side_effects=True, vmem_limit_bytes=60 * 1024 * 1024
        ),
    )(
        market_size, taste_scale, taste_draws.transpose(1, 0, 2).reshape(n_m * K, R), type_weight,
        product_traits.transpose(2, 0, 1), product_firm, mean_utility, market_share,
        loyalty, firm_order.reshape(firms // LANES, LANES), firm_share,
    )


def solution(mesh):
    both = ("mkt", "grp")
    placed = (
        P(both, None), P(both, None), P(both, None, None), P(both, None, None), P(),
        P(both, None), P(both), P(both, None), P(), P(both, None), P(),
    )
    return jax.shard_map(
        functools.partial(local, mesh.shape["mkt"], mesh.shape["grp"]),
        mesh=mesh,
        in_specs=placed,
        out_specs=(P(both, None), P(both, None)),
        check_vma=False,
    )
```

time: 88.1 us -> 77.1 us (0.88)
  Pallas kernels: 84.5 us -> 73.5 us
    pallas_call x1, Pallas kernels: 84.5 us -> 73.5 us  [local(): pl.pallas_call(functools.partial(kernel, dims), out_shape=(jax.ShapeDtype...]
where the time goes in v1:
time: 77.1 us; the launch traced here: 76.9 us
  Pallas kernels  73.5 us (95%)
  local copies, waits for them, and re-layouts  2.77 us (4%)
    pallas_call x1, Pallas kernels, local(): pl.pallas_call(functools.partial(kernel, dims), out_shape=(jax.ShapeDtype...  73.5 us
    unnamed x2, local copies, waits for them, and re-layouts  2.77 us

profile of v1, /device:TPU:0, one launch (start us, length us, event | category | flops | bytes accessed | tf_op | source)
XLA Modules:
  0.0 76.9 jit_solution(9687941347345816530)
XLA Ops:
  0.6 73.5 %shard_map.122 = (f32[16,64]{1,0:T(8,128)}, f32[16,1024]{1,0:T(8,128)}) custom-call(f32[16]{0:T(128)} %size_h.1, f32[5]{0:T(128)} %scale_h.1, f32[80,1024]{1,0:T(8,128)} %bitcast.5, f32[16,1024]{1,0:T(8,128)} %weight_h.1, f32[5,16,64]{2,1,0:T(8,128)} %bitcast.6, s32[16,64]{1,0:T(8,128)} %firm_h.1, f32[16,64]{1,0:T(8,128)} %mean_h.1, f32[16,64]{1,0:T(8,128)} %share_own_h.1, ...), custom_call_target="tpu_custom_call" | custom-call | tf_op jit(solution)/shard_map/pallas_call | solution.py:503
  74.1 1.3 %copy.15 = f32[16,64]{1,0:T(8,128)} copy(f32[16,64]{1,0:T(8,128)} %get-tuple-element.4) | data formatting | bytes 8192
  75.4 1.5 %copy.16 = f32[16,1024]{1,0:T(8,128)} copy(f32[16,1024]{1,0:T(8,128)} %get-tuple-element.5) | data formatting | bytes 131072

commit v2 on v1

v2 whole, which is shorter than its diff:
```python
import functools

import jax
import jax.numpy as jnp
from jax import lax
from jax.experimental import pallas as pl
from jax.experimental.pallas import tpu as pltpu
from jax.sharding import PartitionSpec as P

ITERS = 3
FLAGS = 11 + 6 * ITERS + 5 * (ITERS - 1)
LANES = 128
MESH = pl.DeviceIdType.MESH

clip_target = 0.5
norm_eps = 1e-06

scope = jax.named_scope


def columns(row):
    return jnp.broadcast_to(row, (LANES, LANES)).T


def split_hi_lo(x):
    hi = x.astype(jnp.bfloat16)
    lo = (x - hi.astype(jnp.float32)).astype(jnp.bfloat16)
    return hi, lo


def xor(x, d, size):
    out = x
    bit = 1
    while bit < size:
        out = out + ((d // bit) % 2) * (1 - 2 * ((x // bit) % 2)) * bit
        bit *= 2
    return out


def kernel(
    dims,
    size_h, scale_h, draws_h, weight_h, traits_h, firm_h, mean_h, share_own_h, loy_h, order_h, share_h,
    mean_out, loy_out,
    size_ref, scale_ref, weight_ref, traits_ref, firm_ref, mean_ref, share_own_ref, order_ref, share_v,
    blk, loy, means, tbl, tq, tmass, tm_own,
    mass_own, lmat, rmat, one_hot, util, near_gap, col, order_col, order_row, table_hl, weighted_e, weighted_o,
    acc_e, acc_o,
    sums, sums_in, totals, totals_in, gap, squares, squares_in, old, old_in, last, last_in,
    in_s, blk_s, sem,
):
    mkt, grp, rb, groups, n_m, J, K, firms, owned, R = dims
    n = mkt * grp
    rows = n_m * J
    tiles = rows // LANES
    pair = LANES // J
    qr = firms // groups
    half = groups // 2
    near = half * qr
    pairs = rb // 2
    a = lax.axis_index("mkt")
    b = lax.axis_index("grp")
    ao, ai = a // rb, a % rb
    q_me = ao * grp + b
    me = a * grp + b

    def type_lane(d):
        return xor(ai, d, rb)

    def type_device(d):
        return (ao * rb + xor(ai, d, rb), b)

    def market_device(j):
        q = xor(q_me, j, groups)
        return ((q // grp) * rb + ai, q % grp)

    def lanes_of(p):
        return pl.ds(pl.multiple_of(p * LANES, LANES), LANES)

    names = {}

    def flag(*key):
        return sem.at[names.setdefault(key, len(names))]

    def send(src, dst, out_sem, in_sem, device):
        pltpu.make_async_remote_copy(
            src_ref=src, dst_ref=dst, send_sem=out_sem, recv_sem=in_sem, device_id=device, device_id_type=MESH,
        ).start()

    def arrive(ref, in_sem):
        pltpu.make_async_copy(ref, ref, in_sem).wait()

    m0 = n_m * K
    f0 = m0 + n_m

    def info_row(d, k, i):
        at = f0 + k * tiles + i
        return blk[d, at:at + 1, :]

    def pack(x):
        return jnp.concatenate([x[i * tiles:(i + 1) * tiles, :] for i in range(pair)], axis=1)

    inputs = {}
    for at, (key, src, dst) in enumerate((
        ("weight", weight_h, weight_ref), ("traits", traits_h, traits_ref), ("firm", firm_h, firm_ref),
        ("mean", mean_h, mean_ref), ("size", size_h, size_ref), ("scale", scale_h, scale_ref),
        ("draws", draws_h.at[:, lanes_of(ai)], blk.at[0, :m0]), ("loy", loy_h.at[:, lanes_of(ai)], loy.at[0]),
        ("order", order_h, order_ref), ("share_own", share_own_h, share_own_ref),
        ("share", share_h.at[:, lanes_of(ai)], share_v),
    )):
        inputs[key] = pltpu.make_async_copy(src, dst, in_s.at[at])
        inputs[key].start()

    barrier = pltpu.get_barrier_semaphore()

    @pl.loop(1, n)
    def _(d):
        t = (me + d) % n
        pl.semaphore_signal(barrier, inc=1, device_id=(t // grp, t % grp), device_id_type=MESH)

    for key in ("weight", "traits", "firm", "mean", "size", "scale"):
        inputs[key].wait()
    for k in range(K):
        blk[0, f0 + k * tiles:f0 + (k + 1) * tiles, :] = pack(traits_ref[k] * scale_ref[k])
    blk[0, f0 + K * tiles:f0 + (K + 1) * tiles, :] = pack(firm_ref[...].astype(jnp.float32))
    mean_now = pack(mean_ref[...])
    blk[0, f0 + (K + 1) * tiles:, :] = mean_now
    for m in range(n_m):
        mass_own[m:m + 1, :] = weight_ref[m:m + 1, :] * size_ref[m]

    with scope("bar"):
        pl.semaphore_wait(barrier, n - 1)

    for d in range(1, rb):
        send(loy_h.at[:, lanes_of(type_lane(d))], loy.at[d], flag("loy", 0), flag("loy", 1), type_device(d))
    for d in range(1, rb):
        device = type_device(d)
        lanes = lanes_of(type_lane(d))
        send(draws_h.at[:, lanes], blk.at[d, :m0], flag("blk", 0), blk_s.at[d], device)
        send(blk.at[0, f0:], blk.at[d, f0:], flag("blk", 0), blk_s.at[d], device)
        send(mass_own.at[:, lanes], blk.at[d, m0:f0], flag("blk", 0), blk_s.at[d], device)

    blk[0, m0:f0, :] = mass_own[:, lanes_of(ai)]
    weighted_o[:, (pairs - 1) * rows:] = jnp.zeros_like(weighted_o[:, (pairs - 1) * rows:])
    acc_e[...] = jnp.zeros_like(acc_e)
    acc_o[...] = jnp.zeros_like(acc_o)

    for key in ("order", "draws", "loy"):
        inputs[key].wait()
    for i in range(firms // LANES):
        col[i * LANES:(i + 1) * LANES, :] = columns(order_ref[i:i + 1, :].astype(jnp.float32))
    for j in range(groups):
        q = xor(q_me, j, groups)
        for d in range(rb):
            src = (((q // grp) * rb + xor(ai, d, rb)) * grp + q % grp) * owned
            dst = (j * rb + d) * owned
            order_col[dst:dst + owned, :] = col[pl.ds(pl.multiple_of(src, owned), owned), :]
    for i in range(firms // LANES):
        order_row[0:1, i * LANES:(i + 1) * LANES] = order_col[i * LANES:(i + 1) * LANES, :].T[0:1, :]

    kk = n_m * K
    row = lax.broadcasted_iota(jnp.int32, (n_m, LANES), 0)
    lane = lax.broadcasted_iota(jnp.int32, (n_m, LANES), 1)
    offset = row - (lane // J) * tiles
    zero = jnp.zeros((n_m, LANES), jnp.float32)
    rmat[kk:, :] = jnp.zeros_like(rmat[kk:, :])
    rmat[2 * kk:, :LANES] = jnp.ones_like(rmat[2 * kk:, :LANES])

    weighted = (weighted_e, weighted_o)

    def rows_of(d, r0, count):
        return pl.ds(pl.multiple_of(((d % 2) * pairs + d // 2) * rows + r0, LANES), count)

    def spread(part, where):
        return jnp.where(where, jnp.broadcast_to(part.astype(jnp.float32), (n_m, LANES)), zero).astype(jnp.bfloat16)

    def prepare(d):
        hi, lo = split_hi_lo(blk[d, :m0, :])
        rmat[:kk, :LANES] = hi
        rmat[:kk, LANES:] = lo
        rmat[kk:2 * kk, :LANES] = hi
        for i in range(tiles):
            here = offset == i
            at = slice(i * LANES, (i + 1) * LANES)
            for k in range(K):
                hi, lo = split_hi_lo(info_row(d, k, i))
                lmat[k * n_m:(k + 1) * n_m, at] = spread(hi, here)
                lmat[kk + k * n_m:kk + (k + 1) * n_m, at] = spread(lo, here)
            rest = info_row(d, K + 1, i)
            for s in range(3):
                hi = rest.astype(jnp.bfloat16)
                rest = rest - hi.astype(jnp.float32)
                lmat[2 * kk + s * n_m:2 * kk + (s + 1) * n_m, at] = spread(hi, here)
        both = lax.dot_general(
            lmat[...], rmat[...], (((0,), (0,)), ((), ())), preferred_element_type=jnp.float32
        )
        util[rows_of(d, 0, rows), :] = both[:, :LANES] + both[:, LANES:]
        for i in range(tiles):
            firm_col = columns(info_row(d, K, i))
            for f in range(firms // LANES):
                one_hot[rows_of(d, i * LANES, LANES), f * LANES:(f + 1) * LANES] = (
                    firm_col == order_row[0:1, f * LANES:(f + 1) * LANES]
                ).astype(jnp.float32).astype(jnp.bfloat16)

    with scope("prep0"):
        prepare(0)

    with scope("arr_loy"):
        arrive(loy.at[1:], flag("loy", 1))
    for d in range(rb):
        tq[d * owned:(d + 1) * owned, :] = loy[d]
    for j in range(1, groups):
        send(tq, tbl.at[j], flag("tq", 0), flag("tq", 1), market_device(j))
    tbl[0] = tq[...]

    def arrive_inputs(d):
        arrive(blk.at[d], blk_s.at[d])

    first = rb // 2

    @pl.loop(1, first)
    def _(d):
        with scope("arr_a"):
            arrive_inputs(d)
        with scope("prep_a"):
            prepare(d)

    with scope("share"):
        inputs["share"].wait()
        inputs["share_own"].wait()
        mine_col = order_col[:qr, :]
        number = lax.broadcasted_iota(jnp.int32, (qr, LANES), 1).astype(jnp.float32)
        my_share = jnp.zeros((qr, LANES), jnp.float32)
        for i in range(firms // LANES):
            pick = (mine_col == number + float(i * LANES)).astype(jnp.float32)
            my_share += jnp.dot(
                pick, share_v[i * LANES:(i + 1) * LANES, :],
                precision=lax.Precision.HIGHEST, preferred_element_type=jnp.float32,
            )
        my_share = jnp.log(my_share)
        base = jnp.log(share_own_ref[...]) + jnp.log(jnp.sum(mass_own[...], axis=1, keepdims=True))
        base = pack(base)

    with scope("arr_tbl"):
        arrive(tbl.at[1:], flag("tq", 1))

    def split_into(j, value):
        hi, lo = split_hi_lo(value)
        table_hl[j * qr:(j + 1) * qr, :LANES] = hi
        table_hl[j * qr:(j + 1) * qr, LANES:] = lo

    for j in range(groups):
        split_into(j, tbl[j])

    per_block = 2
    block = per_block * LANES

    def gather(d, r0, begin, end):
        both = jnp.dot(
            one_hot[rows_of(d, r0, block), begin:end], table_hl[begin:end, :], preferred_element_type=jnp.float32
        )
        return both[:, :LANES] + both[:, LANES:]

    def shares(it, i, par, clip, other):
        d = 2 * i + par
        moved = None
        for h in range(rows // block):
            r0 = h * block
            at = rows_of(d, r0, block)
            if it == 0:
                u = util[at, :] + gather(d, r0, 0, firms)
            else:
                u = util[at, :] + clip * (near_gap[at, :] + gather(d, r0, near, firms))
            if it < ITERS - 1:
                util[at, :] = u
            chunk = far_part(other, 1 - par, r0, block)
            moved = chunk if moved is None else moved + chunk
            expu = jnp.exp(u)
            for c in range(per_block):
                t = h * per_block + c
                parts = []
                for s in range(pair):
                    part = expu[c * LANES + s * J:c * LANES + (s + 1) * J, :]
                    m = s * tiles + t
                    parts.append(
                        part * (blk[d, m0 + m:m0 + m + 1, :] / (1.0 + jnp.sum(part, axis=0, keepdims=True)))
                    )
                bought = jnp.concatenate(parts, axis=0).T
                sums[it, d, t:t + 1, :] = jnp.sum(bought, axis=0, keepdims=True)
                hi, lo = split_hi_lo(bought)
                lanes = pl.ds(pl.multiple_of(i * rows + t * LANES, LANES), LANES)
                weighted[par][:LANES, lanes] = hi
                weighted[par][LANES:, lanes] = lo
        return moved

    def far_part(i, par, r0, count):
        lanes = pl.ds(pl.multiple_of(i * rows + r0, LANES), count)
        part = jnp.dot(
            weighted[par][:, lanes], one_hot[rows_of(2 * i + par, r0, count), near:],
            preferred_element_type=jnp.float32,
        )
        return part[:LANES, :] + part[LANES:, :]

    def pair_step(it, s, clip, ready):
        i = s if it == 0 else pairs - 1 - s
        prev = (s + pairs - 1) % pairs if it == 0 else (pairs - s) % pairs
        started = s > 0
        ready(2 * i)
        part = shares(it, i, 0, clip, prev)
        acc_o[...] = jnp.where(started, acc_o[...] + part, 0.0)
        ready(2 * i + 1)
        part = shares(it, i, 1, clip, i)
        acc_e[...] = jnp.where(started, acc_e[...], 0.0) + part
        send_sums(it, 2 * i + 1)

        @pl.when(i > 0)
        def _():
            send_sums(it, 2 * i)

    def send_sums(it, d):
        send(sums.at[it, d], sums_in.at[it, d], flag("sums", it, 0), flag("sums", it, 1), type_device(d))

    def by_firm(x):
        return jnp.concatenate([x[:, i * LANES:(i + 1) * LANES].T for i in range(near // LANES)], axis=0)

    def far_totals(it):
        acc = by_firm(acc_e[...] + acc_o[...] + far_part(pairs - 1 if it == 0 else 0, 1, 0, rows))
        for j in range(half):
            totals[it, half + j] = acc[j * qr:(j + 1) * qr, :]

    def near_totals(it):
        acc = None
        for par in range(2):
            part = jnp.dot(
                weighted[par][...], one_hot[par * pairs * rows:(par + 1) * pairs * rows, :near],
                preferred_element_type=jnp.float32,
            )
            part = by_firm(part[:LANES, :] + part[LANES:, :])
            acc = part if acc is None else acc + part
        for j in range(half):
            totals[it, j] = acc[j * qr:(j + 1) * qr, :]

    clip = None
    log_mass = None
    for it in range(ITERS):
        final = it == ITERS - 1
        if it == 0:
            with scope("sh_a"):
                @pl.loop(0, first // 2)
                def _(i):
                    pair_step(0, i, None, lambda d: None)

            def ready(d):
                with scope("arr_b"):
                    arrive_inputs(d)
                prepare(d)

            @pl.loop(first // 2, pairs)
            def _(i):
                pair_step(0, i, None, ready)

            tm_own[...] = jnp.zeros_like(tm_own)
            for d in range(rb):
                tm_own[...] += jnp.sum(blk[d, m0:f0, :], axis=0, keepdims=True)
            for j in range(1, groups):
                send(tm_own, tmass.at[j], flag("tm", 0), flag("tm", 1), market_device(j))
            tmass[0] = tm_own[...]
        else:
            with scope("shares%d" % it):
                @pl.loop(0, pairs)
                def _(i):
                    pair_step(it, i, clip, lambda d: None)

        sums_in[it, 0] = sums[it, 0]

        with scope("far%d" % it):
            far_totals(it)
        for j in range(half, groups):
            send(totals.at[it, j], totals_in.at[it, j], flag("totals", it, 0), flag("totals", it, 1), market_device(j))
        with scope("near%d" % it):
            near_totals(it)
        for j in range(1, half):
            send(totals.at[it, j], totals_in.at[it, j], flag("totals", it, 0), flag("totals", it, 1), market_device(j))
        totals_in[it, 0] = totals[it, 0]

        if final:
            for d in range(rb):
                old[d] = tbl[0, d * owned:(d + 1) * owned, :]
            for d in range(1, rb):
                send(old.at[d], old_in.at[d], flag("old", 0), flag("old", 1), type_device(d))
            old_in[0] = old[0]

        if it == 0:
            arrive(tmass.at[1:], flag("tm", 1))
            log_mass = jnp.log(jnp.sum(tmass[...], axis=0))

        def settle_means(mean_now):
            with scope("arr_sums%d" % it):
                arrive(sums_in.at[it, 1:], flag("sums", it, 1))
            step = base - jnp.log(jnp.sum(sums_in[it], axis=0))
            mean_now = mean_now + step
            if final:
                for i in range(pair):
                    mean_out[i * tiles:(i + 1) * tiles, :] = mean_now[:, i * J:(i + 1) * J]
            else:
                means[it, 0] = step
                for d in range(1, rb):
                    send(means.at[it, 0], means.at[it, d], flag("means", it, 0), flag("means", it, 1), type_device(d))
            return mean_now

        if it:
            mean_now = settle_means(mean_now)
        with scope("arr_tot%d" % it):
            arrive(totals_in.at[it, 1:], flag("totals", it, 1))
        gap_mine = my_share - (jnp.log(jnp.sum(totals_in[it], axis=0)) - log_mass)
        squares[it] = jnp.sum(gap_mine * gap_mine, axis=0, keepdims=True)

        @pl.loop(1, n)
        def _(d):
            t = (me + d) % n
            send(
                squares.at[it], squares_in.at[it, d - 1], flag("sq", it, 0), flag("sq", it, 1), (t // grp, t % grp)
            )

        if final:
            for d in range(rb):
                last[d] = gap_mine[d * owned:(d + 1) * owned, :]
            for d in range(1, rb):
                send(last.at[d], last_in.at[d], flag("last", 0), flag("last", 1), type_device(d))
            last_in[0] = last[0]
        else:
            gap[it, 0] = gap_mine
            for j in [*range(half, groups), *range(1, half)]:
                send(gap.at[it, 0], gap.at[it, j], flag("gap", it, 0), flag("gap", it, 1 + j // half), market_device(j))
            if it == 0:
                mean_now = settle_means(mean_now)
            with scope("arr_gapn%d" % it):
                split_into(0, gap_mine)
                arrive(gap.at[it, 1:half], flag("gap", it, 1))
                for j in range(1, half):
                    split_into(j, gap[it, j])

            with scope("gnear%d" % it):
                @pl.loop(0, pairs)
                def _(i):
                    for par in range(2):
                        at = rows_of(2 * i + par, 0, rows)
                        both = jnp.dot(one_hot[at, :near], table_hl[:near, :], preferred_element_type=jnp.float32)
                        near_gap[at, :] = both[:, :LANES] + both[:, LANES:]

            with scope("arr_mean%d" % it):
                arrive(means.at[it, 1:], flag("means", it, 1))

            with scope("addmean%d" % it):
                @pl.loop(0, pairs)
                def _(i):
                    for par in range(2):
                        for t in range(tiles):
                            at = rows_of(2 * i + par, t * LANES, LANES)
                            util[at, :] = util[at, :] + columns(means[it, 2 * i + par, t:t + 1, :])

            with scope("arr_gap%d" % it):
                arrive(gap.at[it, half:], flag("gap", it, 2))
                for j in range(half, groups):
                    split_into(j, gap[it, j])

        with scope("arr_sq%d" % it):
            arrive(squares_in.at[it], flag("sq", it, 1))
        total = jnp.sum(jnp.sum(squares_in[it], axis=0) + squares[it], axis=1, keepdims=True)
        clip = jnp.minimum(1.0, clip_target / jnp.sqrt(total / (firms * R) + norm_eps))

        if final:
            with scope("arr_last"):
                arrive(old_in.at[1:], flag("old", 1))
                arrive(last_in.at[1:], flag("last", 1))
            for d in range(rb):
                loy_out[:, lanes_of(type_lane(d))] = old_in[d] + clip * last_in[d]
        else:
            tbl[0] = tbl[0] + clip * gap_mine

    with scope("drain"):
        arrive(loy.at[1:], flag("loy", 0))
        arrive(blk.at[1:], flag("blk", 0))
        arrive(tbl.at[1:], flag("tq", 0))
        arrive(tmass.at[1:], flag("tm", 0))
        arrive(old.at[1:], flag("old", 0))
        arrive(last.at[1:], flag("last", 0))
        for it in range(ITERS):
            arrive(sums.at[it, 1:], flag("sums", it, 0))
            arrive(totals.at[it, 1:], flag("totals", it, 0))
            arrive(squares_in.at[it], flag("sq", it, 0))
            if it < ITERS - 1:
                arrive(means.at[it, 1:], flag("means", it, 0))
                arrive(gap.at[it, 1:], flag("gap", it, 0))
    assert len(names) == FLAGS


def local(
    mkt, grp,
    mean_utility, market_share, product_traits, taste_draws, taste_scale, type_weight,
    market_size, product_firm, firm_order, loyalty, firm_share,
):
    n_m, J, K = product_traits.shape
    firms, R = firm_share.shape
    owned = loyalty.shape[0]
    rb = R // LANES
    groups = mkt * grp // rb
    rows = n_m * J
    tiles = rows // LANES
    qr = firms // groups
    depth = n_m * (2 * K + 3)

    f32, bf16 = jnp.float32, jnp.bfloat16
    dma = pltpu.SemaphoreType.DMA
    vmem = pltpu.VMEM
    spec = pl.BlockSpec(memory_space=pltpu.VMEM)
    dims = (mkt, grp, rb, groups, n_m, J, K, firms, owned, R)
    scratch = [
        pltpu.SMEM((n_m,), f32),
        pltpu.SMEM((K,), f32),
        vmem((n_m, R), f32),
        vmem((K, n_m, J), f32),
        vmem((n_m, J), jnp.int32),
        vmem((n_m, J), f32),
        vmem((n_m, J), f32),
        vmem((firms // LANES, LANES), jnp.int32),
        vmem((firms, LANES), f32),
        vmem((rb, n_m * (K + 1) + (K + 2) * tiles, LANES), f32),
        vmem((rb, owned, LANES), f32),
        vmem((ITERS - 1, rb, tiles, LANES), f32),
        vmem((groups, qr, LANES), f32),
        vmem((qr, LANES), f32),
        vmem((groups, 1, LANES), f32),
        vmem((1, LANES), f32),
        vmem((n_m, R), f32),
        vmem((depth, rows), bf16),
        vmem((depth, 2 * LANES), bf16),
        vmem((rb * rows, firms), bf16),
        vmem((rb * rows, LANES), f32),
        vmem((rb * rows, LANES), f32),
        vmem((firms, LANES), f32),
        vmem((firms, LANES), f32),
        vmem((1, firms), f32),
        vmem((firms, 2 * LANES), bf16),
        vmem((2 * LANES, rb // 2 * rows), bf16),
        vmem((2 * LANES, rb // 2 * rows), bf16),
        vmem((LANES, firms // 2), f32),
        vmem((LANES, firms // 2), f32),
        vmem((ITERS, rb, tiles, LANES), f32),
        vmem((ITERS, rb, tiles, LANES), f32),
        vmem((ITERS, groups, qr, LANES), f32),
        vmem((ITERS, groups, qr, LANES), f32),
        vmem((ITERS - 1, groups, qr, LANES), f32),
        vmem((ITERS, 1, LANES), f32),
        vmem((ITERS, mkt * grp - 1, 1, LANES), f32),
        vmem((rb, owned, LANES), f32),
        vmem((rb, owned, LANES), f32),
        vmem((rb, owned, LANES), f32),
        vmem((rb, owned, LANES), f32),
        dma((11,)),
        dma((rb,)),
        dma((FLAGS,)),
    ]
    return pl.pallas_call(
        functools.partial(kernel, dims),
        out_shape=(
            jax.ShapeDtypeStruct((n_m, J), f32),
            jax.ShapeDtypeStruct((owned, R), f32),
        ),
        in_specs=[pl.BlockSpec(memory_space=pl.ANY)] * 11,
        out_specs=(spec, spec),
        scratch_shapes=scratch,
        compiler_params=pltpu.CompilerParams(
            collective_id=0, has_side_effects=True, vmem_limit_bytes=60 * 1024 * 1024
        ),
    )(
        market_size, taste_scale, taste_draws.transpose(1, 0, 2).reshape(n_m * K, R), type_weight,
        product_traits.transpose(2, 0, 1), product_firm, mean_utility, market_share,
        loyalty, firm_order.reshape(firms // LANES, LANES), firm_share,
    )


def solution(mesh):
    both = ("mkt", "grp")
    placed = (
        P(both, None), P(both, None), P(both, None, None), P(both, None, None), P(),
        P(both, None), P(both), P(both, None), P(), P(both, None), P(),
    )
    return jax.shard_map(
        functools.partial(local, mesh.shape["mkt"], mesh.shape["grp"]),
        mesh=mesh,
        in_specs=placed,
        out_specs=(P(both, None), P(both, None)),
        check_vma=False,
    )
```

time: 77.1 us -> 69.6 us (0.903)
  Pallas kernels: 73.5 us -> 65.9 us
    pallas_call x1, Pallas kernels: 73.5 us -> 65.9 us  [local(): pl.pallas_call(functools.partial(kernel, dims), out_shape=(jax.ShapeDtype...]
where the time goes in v2:
time: 69.6 us; the launch traced here: 69.4 us
  Pallas kernels  65.9 us (95%)
  local copies, waits for them, and re-layouts  2.77 us (4%)
    pallas_call x1, Pallas kernels, local(): pl.pallas_call(functools.partial(kernel, dims), out_shape=(jax.ShapeDtype...  65.9 us
    unnamed x2, local copies, waits for them, and re-layouts  2.77 us

profile of v2, /device:TPU:0, one launch (start us, length us, event | category | flops | bytes accessed | tf_op | source)
XLA Modules:
  0.0 69.4 jit_solution(5911590049867773084)
XLA Ops:
  0.6 65.9 %shard_map.122 = (f32[16,64]{1,0:T(8,128)}, f32[16,1024]{1,0:T(8,128)}) custom-call(f32[16]{0:T(128)} %size_h.1, f32[5]{0:T(128)} %scale_h.1, f32[80,1024]{1,0:T(8,128)} %bitcast.5, f32[16,1024]{1,0:T(8,128)} %weight_h.1, f32[5,16,64]{2,1,0:T(8,128)} %bitcast.6, s32[16,64]{1,0:T(8,128)} %firm_h.1, f32[16,64]{1,0:T(8,128)} %mean_h.1, f32[16,64]{1,0:T(8,128)} %share_own_h.1, ...), custom_call_target="tpu_custom_call" | custom-call | tf_op jit(solution)/shard_map/pallas_call | solution.py:563
  66.6 1.3 %copy.15 = f32[16,64]{1,0:T(8,128)} copy(f32[16,64]{1,0:T(8,128)} %get-tuple-element.4) | data formatting | bytes 8192
  67.9 1.5 %copy.16 = f32[16,1024]{1,0:T(8,128)} copy(f32[16,1024]{1,0:T(8,128)} %get-tuple-element.5) | data formatting | bytes 131072

commit v3 on v2

--- a/solution.py
+++ b/solution.py
@@ -8,7 +8,7 @@
 from jax.sharding import PartitionSpec as P
 
 ITERS = 3
-FLAGS = 11 + 6 * ITERS + 5 * (ITERS - 1)
+FLAGS = 12 + 6 * ITERS + 5 * (ITERS - 1)
 LANES = 128
 MESH = pl.DeviceIdType.MESH
 
@@ -42,11 +42,11 @@
     size_h, scale_h, draws_h, weight_h, traits_h, firm_h, mean_h, share_own_h, loy_h, order_h, share_h,
     mean_out, loy_out,
     size_ref, scale_ref, weight_ref, traits_ref, firm_ref, mean_ref, share_own_ref, order_ref, share_v,
-    blk, loy, means, tbl, tq, tmass, tm_own,
-    mass_own, lmat, rmat, one_hot, util, near_gap, col, order_col, order_row, table_hl, weighted_e, weighted_o,
+    blk, info, loy, means, tbl, tq, tmass, tm_own,
+    mass_own, lmat, rmats, one_hot, util, near_gap, col, order_col, order_row, table_hl, weighted_e, weighted_o,
     acc_e, acc_o,
     sums, sums_in, totals, totals_in, gap, squares, squares_in, old, old_in, last, last_in,
-    in_s, blk_s, sem,
+    in_s, blk_s, info_s, sem,
 ):
     mkt, grp, rb, groups, n_m, J, K, firms, owned, R = dims
     n = mkt * grp
@@ -90,11 +90,10 @@
         pltpu.make_async_copy(ref, ref, in_sem).wait()
 
     m0 = n_m * K
-    f0 = m0 + n_m
 
     def info_row(d, k, i):
-        at = f0 + k * tiles + i
-        return blk[d, at:at + 1, :]
+        at = k * tiles + i
+        return info[d, at:at + 1, :]
 
     def pack(x):
         return jnp.concatenate([x[i * tiles:(i + 1) * tiles, :] for i in range(pair)], axis=1)
@@ -120,10 +119,10 @@
     for key in ("weight", "traits", "firm", "mean", "size", "scale"):
         inputs[key].wait()
     for k in range(K):
-        blk[0, f0 + k * tiles:f0 + (k + 1) * tiles, :] = pack(traits_ref[k] * scale_ref[k])
-    blk[0, f0 + K * tiles:f0 + (K + 1) * tiles, :] = pack(firm_ref[...].astype(jnp.float32))
+        info[0, k * tiles:(k + 1) * tiles, :] = pack(traits_ref[k] * scale_ref[k])
+    info[0, K * tiles:(K + 1) * tiles, :] = pack(firm_ref[...].astype(jnp.float32))
     mean_now = pack(mean_ref[...])
-    blk[0, f0 + (K + 1) * tiles:, :] = mean_now
+    info[0, (K + 1) * tiles:, :] = mean_now
     for m in range(n_m):
         mass_own[m:m + 1, :] = weight_ref[m:m + 1, :] * size_ref[m]
 
@@ -132,14 +131,21 @@
 
     for d in range(1, rb):
         send(loy_h.at[:, lanes_of(type_lane(d))], loy.at[d], flag("loy", 0), flag("loy", 1), type_device(d))
+    for d in [1, *range(2, rb, 2)]:
+        send(info.at[0], info.at[d], flag("info", 0), info_s.at[d], type_device(d))
     for d in range(1, rb):
         device = type_device(d)
         lanes = lanes_of(type_lane(d))
         send(draws_h.at[:, lanes], blk.at[d, :m0], flag("blk", 0), blk_s.at[d], device)
-        send(blk.at[0, f0:], blk.at[d, f0:], flag("blk", 0), blk_s.at[d], device)
-        send(mass_own.at[:, lanes], blk.at[d, m0:f0], flag("blk", 0), blk_s.at[d], device)
-
-    blk[0, m0:f0, :] = mass_own[:, lanes_of(ai)]
+        send(mass_own.at[:, lanes], blk.at[d, m0:], flag("blk", 0), blk_s.at[d], device)
+
+    def arrive_info(d):
+        arrive(info.at[d], info_s.at[d])
+
+    def hand_on(d):
+        send(info.at[d], info.at[d + 1], flag("info", 0), info_s.at[d + 1], type_device(1))
+
+    blk[0, m0:, :] = mass_own[:, lanes_of(ai)]
     weighted_o[:, (pairs - 1) * rows:] = jnp.zeros_like(weighted_o[:, (pairs - 1) * rows:])
     acc_e[...] = jnp.zeros_like(acc_e)
     acc_o[...] = jnp.zeros_like(acc_o)
@@ -162,8 +168,8 @@
     lane = lax.broadcasted_iota(jnp.int32, (n_m, LANES), 1)
     offset = row - (lane // J) * tiles
     zero = jnp.zeros((n_m, LANES), jnp.float32)
-    rmat[kk:, :] = jnp.zeros_like(rmat[kk:, :])
-    rmat[2 * kk:, :LANES] = jnp.ones_like(rmat[2 * kk:, :LANES])
+    rmats[:, kk:, :] = jnp.zeros_like(rmats[:, kk:, :])
+    rmats[:, 2 * kk:, :LANES] = jnp.ones_like(rmats[:, 2 * kk:, :LANES])
 
     weighted = (weighted_e, weighted_o)
 
@@ -173,27 +179,19 @@
     def spread(part, where):
         return jnp.where(where, jnp.broadcast_to(part.astype(jnp.float32), (n_m, LANES)), zero).astype(jnp.bfloat16)
 
-    def prepare(d):
-        hi, lo = split_hi_lo(blk[d, :m0, :])
-        rmat[:kk, :LANES] = hi
-        rmat[:kk, LANES:] = lo
-        rmat[kk:2 * kk, :LANES] = hi
+    def build(d):
         for i in range(tiles):
             here = offset == i
             at = slice(i * LANES, (i + 1) * LANES)
             for k in range(K):
                 hi, lo = split_hi_lo(info_row(d, k, i))
-                lmat[k * n_m:(k + 1) * n_m, at] = spread(hi, here)
-                lmat[kk + k * n_m:kk + (k + 1) * n_m, at] = spread(lo, here)
+                lmat[d, k * n_m:(k + 1) * n_m, at] = spread(hi, here)
+                lmat[d, kk + k * n_m:kk + (k + 1) * n_m, at] = spread(lo, here)
             rest = info_row(d, K + 1, i)
             for s in range(3):
                 hi = rest.astype(jnp.bfloat16)
                 rest = rest - hi.astype(jnp.float32)
-                lmat[2 * kk + s * n_m:2 * kk + (s + 1) * n_m, at] = spread(hi, here)
-        both = lax.dot_general(
-            lmat[...], rmat[...], (((0,), (0,)), ((), ())), preferred_element_type=jnp.float32
-        )
-        util[rows_of(d, 0, rows), :] = both[:, :LANES] + both[:, LANES:]
+                lmat[d, 2 * kk + s * n_m:2 * kk + (s + 1) * n_m, at] = spread(hi, here)
         for i in range(tiles):
             firm_col = columns(info_row(d, K, i))
             for f in range(firms // LANES):
@@ -201,29 +199,20 @@
                     firm_col == order_row[0:1, f * LANES:(f + 1) * LANES]
                 ).astype(jnp.float32).astype(jnp.bfloat16)
 
+    def taste(d, par):
+        rmat = rmats.at[par]
+        hi, lo = split_hi_lo(blk[d, :m0, :])
+        rmat[:kk, :LANES] = hi
+        rmat[:kk, LANES:] = lo
+        rmat[kk:2 * kk, :LANES] = hi
+        both = lax.dot_general(
+            lmat[d], rmat[...], (((0,), (0,)), ((), ())), preferred_element_type=jnp.float32
+        )
+        util[rows_of(d, 0, rows), :] = both[:, :LANES] + both[:, LANES:]
+
     with scope("prep0"):
-        prepare(0)
-
-    with scope("arr_loy"):
-        arrive(loy.at[1:], flag("loy", 1))
-    for d in range(rb):
-        tq[d * owned:(d + 1) * owned, :] = loy[d]
-    for j in range(1, groups):
-        send(tq, tbl.at[j], flag("tq", 0), flag("tq", 1), market_device(j))
-    tbl[0] = tq[...]
-
-    def arrive_inputs(d):
-        arrive(blk.at[d], blk_s.at[d])
-
-    first = rb // 2
-
-    @pl.loop(1, first)
-    def _(d):
-        with scope("arr_a"):
-            arrive_inputs(d)
-        with scope("prep_a"):
-            prepare(d)
-
+        build(0)
+        taste(0, 0)
     with scope("share"):
         inputs["share"].wait()
         inputs["share_own"].wait()
@@ -239,6 +228,50 @@
         my_share = jnp.log(my_share)
         base = jnp.log(share_own_ref[...]) + jnp.log(jnp.sum(mass_own[...], axis=1, keepdims=True))
         base = pack(base)
+
+    with scope("arr_i2"):
+        arrive_info(2)
+    hand_on(2)
+    with scope("arr_i1"):
+        arrive_info(1)
+
+    @pl.loop(1, 3)
+    def _(d):
+        with scope("build12"):
+            build(d)
+
+    with scope("arr_loy"):
+        arrive(loy.at[1:], flag("loy", 1))
+    for d in range(rb):
+        tq[d * owned:(d + 1) * owned, :] = loy[d]
+    for j in range(1, groups):
+        send(tq, tbl.at[j], flag("tq", 0), flag("tq", 1), market_device(j))
+    tbl[0] = tq[...]
+
+    @pl.loop(2, pairs)
+    def _(i):
+        with scope("arr_ie"):
+            arrive_info(2 * i)
+        hand_on(2 * i)
+        build(2 * i)
+
+    @pl.loop(1, pairs)
+    def _(i):
+        with scope("arr_io"):
+            arrive_info(2 * i + 1)
+        build(2 * i + 1)
+
+    def arrive_inputs(d):
+        arrive(blk.at[d], blk_s.at[d])
+
+    first = rb // 2
+
+    @pl.loop(1, first)
+    def _(d):
+        with scope("arr_a"):
+            arrive_inputs(d)
+        with scope("prep_a"):
+            taste(d, 0)
 
     with scope("arr_tbl"):
         arrive(tbl.at[1:], flag("tq", 1))
@@ -304,17 +337,20 @@
         i = s if it == 0 else pairs - 1 - s
         prev = (s + pairs - 1) % pairs if it == 0 else (pairs - s) % pairs
         started = s > 0
-        ready(2 * i)
+        ready(i)
         part = shares(it, i, 0, clip, prev)
         acc_o[...] = jnp.where(started, acc_o[...] + part, 0.0)
-        ready(2 * i + 1)
         part = shares(it, i, 1, clip, i)
         acc_e[...] = jnp.where(started, acc_e[...], 0.0) + part
         send_sums(it, 2 * i + 1)
 
-        @pl.when(i > 0)
-        def _():
-            send_sums(it, 2 * i)
+        if isinstance(i, int):
+            if i:
+                send_sums(it, 2 * i)
+        else:
+            @pl.when(i > 0)
+            def _():
+                send_sums(it, 2 * i)
 
     def send_sums(it, d):
         send(sums.at[it, d], sums_in.at[it, d], flag("sums", it, 0), flag("sums", it, 1), type_device(d))
@@ -349,10 +385,13 @@
                 def _(i):
                     pair_step(0, i, None, lambda d: None)
 
-            def ready(d):
+            def ready(i):
                 with scope("arr_b"):
-                    arrive_inputs(d)
-                prepare(d)
+                    for par in range(2):
+                        arrive_inputs(2 * i + par)
+                with scope("taste_b"):
+                    for par in range(2):
+                        taste(2 * i + par, par)
 
             @pl.loop(first // 2, pairs)
             def _(i):
@@ -360,14 +399,13 @@
 
             tm_own[...] = jnp.zeros_like(tm_own)
             for d in range(rb):
-                tm_own[...] += jnp.sum(blk[d, m0:f0, :], axis=0, keepdims=True)
+                tm_own[...] += jnp.sum(blk[d, m0:, :], axis=0, keepdims=True)
             for j in range(1, groups):
                 send(tm_own, tmass.at[j], flag("tm", 0), flag("tm", 1), market_device(j))
             tmass[0] = tm_own[...]
         else:
             with scope("shares%d" % it):
-                @pl.loop(0, pairs)
-                def _(i):
+                for i in range(pairs):
                     pair_step(it, i, clip, lambda d: None)
 
         sums_in[it, 0] = sums[it, 0]
@@ -479,6 +517,7 @@
 
     with scope("drain"):
         arrive(loy.at[1:], flag("loy", 0))
+        arrive(info.at[1:], flag("info", 0))
         arrive(blk.at[1:], flag("blk", 0))
         arrive(tbl.at[1:], flag("tq", 0))
         arrive(tmass.at[1:], flag("tm", 0))
@@ -524,7 +563,8 @@
         vmem((n_m, J), f32),
         vmem((firms // LANES, LANES), jnp.int32),
         vmem((firms, LANES), f32),
-        vmem((rb, n_m * (K + 1) + (K + 2) * tiles, LANES), f32),
+        vmem((rb, n_m * (K + 1), LANES), f32),
+        vmem((rb, (K + 2) * tiles, LANES), f32),
         vmem((rb, owned, LANES), f32),
         vmem((ITERS - 1, rb, tiles, LANES), f32),
         vmem((groups, qr, LANES), f32),
@@ -532,8 +572,8 @@
         vmem((groups, 1, LANES), f32),
         vmem((1, LANES), f32),
         vmem((n_m, R), f32),
-        vmem((depth, rows), bf16),
-        vmem((depth, 2 * LANES), bf16),
+        vmem((rb, depth, rows), bf16),
+        vmem((2, depth, 2 * LANES), bf16),
         vmem((rb * rows, firms), bf16),
         vmem((rb * rows, LANES), f32),
         vmem((rb * rows, LANES), f32),
@@ -558,13 +598,14 @@
         vmem((rb, owned, LANES), f32),
         dma((11,)),
         dma((rb,)),
+        dma((rb,)),
         dma((FLAGS,)),
     ]
     return pl.pallas_call(
         functools.partial(kernel, dims),
         out_shape=(
-            jax.ShapeDtypeStruct((n_m, J), f32),
-            jax.ShapeDtypeStruct((owned, R), f32),
+            pltpu.VMEM((n_m, J), f32),
+            pltpu.VMEM((owned, R), f32),
         ),
         in_specs=[pl.BlockSpec(memory_space=pl.ANY)] * 11,
         out_specs=(spec, spec),

time: 69.6 us -> 64 us (0.920)
  Pallas kernels: 65.9 us -> 62 us
  local copies, waits for them, and re-layouts: 2.77 us -> 1.23 us
    pallas_call x1, Pallas kernels: 65.9 us -> 62 us  [local(): pl.pallas_call(functools.partial(kernel, dims), out_shape=(pltpu.VMEM((n_...]
    unnamed x2, local copies, waits for them, and re-layouts: 2.77 us -> 1.23 us
where the time goes in v3:
time: 64 us; the launch traced here: 63.9 us
  Pallas kernels  62 us (97%)
  local copies, waits for them, and re-layouts  1.23 us (2%)
  between operations  0.64 us (1%)
    pallas_call x1, Pallas kernels, local(): pl.pallas_call(functools.partial(kernel, dims), out_shape=(pltpu.VMEM((n_...  62 us

profile of v3, /device:TPU:0, one launch (start us, length us, event | category | flops | bytes accessed | tf_op | source)
XLA Modules:
  0.0 63.9 jit_solution(10634320925796156670)
XLA Ops:
  0.6 62.0 %shard_map.122 = (f32[16,64]{1,0:T(8,128)S(1)}, f32[16,1024]{1,0:T(8,128)S(1)}) custom-call(f32[16]{0:T(128)} %size_h.1, f32[5]{0:T(128)} %scale_h.1, f32[80,1024]{1,0:T(8,128)} %bitcast.5, f32[16,1024]{1,0:T(8,128)} %weight_h.1, f32[5,16,64]{2,1,0:T(8,128)} %bitcast.6, s32[16,64]{1,0:T(8,128)} %firm_h.1, f32[16,64]{1,0:T(8,128)} %mean_h.1, ...), custom_call_target="tpu_custom_call" | custom-call | tf_op jit(solution)/shard_map/pallas_call | solution.py:604
  62.6 0.6 copy.15
  63.2 0.6 copy.16

commit v4 on v3

--- a/solution.py
+++ b/solution.py
@@ -8,7 +8,7 @@
 from jax.sharding import PartitionSpec as P
 
 ITERS = 3
-FLAGS = 12 + 6 * ITERS + 5 * (ITERS - 1)
+FLAGS = 12 + 6 * ITERS + 6 * (ITERS - 1)
 LANES = 128
 MESH = pl.DeviceIdType.MESH
 
@@ -255,18 +255,25 @@
         hand_on(2 * i)
         build(2 * i)
 
+    def arrive_inputs(d):
+        arrive(blk.at[d], blk_s.at[d])
+
+    @pl.loop(1, 3)
+    def _(d):
+        with scope("arr_a"):
+            arrive_inputs(d)
+        with scope("prep_a"):
+            taste(d, 0)
+
     @pl.loop(1, pairs)
     def _(i):
         with scope("arr_io"):
             arrive_info(2 * i + 1)
         build(2 * i + 1)
 
-    def arrive_inputs(d):
-        arrive(blk.at[d], blk_s.at[d])
-
     first = rb // 2
 
-    @pl.loop(1, first)
+    @pl.loop(3, first)
     def _(d):
         with scope("arr_a"):
             arrive_inputs(d)
@@ -381,8 +388,7 @@
         final = it == ITERS - 1
         if it == 0:
             with scope("sh_a"):
-                @pl.loop(0, first // 2)
-                def _(i):
+                for i in range(first // 2):
                     pair_step(0, i, None, lambda d: None)
 
             def ready(i):
@@ -452,12 +458,13 @@
         gap_mine = my_share - (jnp.log(jnp.sum(totals_in[it], axis=0)) - log_mass)
         squares[it] = jnp.sum(gap_mine * gap_mine, axis=0, keepdims=True)
 
-        @pl.loop(1, n)
-        def _(d):
-            t = (me + d) % n
-            send(
-                squares.at[it], squares_in.at[it, d - 1], flag("sq", it, 0), flag("sq", it, 1), (t // grp, t % grp)
-            )
+        def send_squares():
+            @pl.loop(1, n)
+            def _(d):
+                t = (me + d) % n
+                send(
+                    squares.at[it], squares_in.at[it, d - 1], flag("sq", it, 0), flag("sq", it, 1), (t // grp, t % grp)
+                )
 
         if final:
             for d in range(rb):
@@ -465,39 +472,55 @@
             for d in range(1, rb):
                 send(last.at[d], last_in.at[d], flag("last", 0), flag("last", 1), type_device(d))
             last_in[0] = last[0]
+            send_squares()
         else:
             gap[it, 0] = gap_mine
-            for j in [*range(half, groups), *range(1, half)]:
+            for j in [half, *range(1, half)]:
                 send(gap.at[it, 0], gap.at[it, j], flag("gap", it, 0), flag("gap", it, 1 + j // half), market_device(j))
+            send_squares()
             if it == 0:
                 mean_now = settle_means(mean_now)
-            with scope("arr_gapn%d" % it):
-                split_into(0, gap_mine)
-                arrive(gap.at[it, 1:half], flag("gap", it, 1))
+            def add_near():
+                with scope("arr_gapn%d" % it):
+                    split_into(0, gap_mine)
+                    arrive(gap.at[it, 1:half], flag("gap", it, 1))
+                    for j in range(1, half):
+                        split_into(j, gap[it, j])
+
+                with scope("gnear%d" % it):
+                    @pl.loop(0, pairs // 2)
+                    def _(i):
+                        for par in range(4):
+                            at = rows_of(4 * i + par, 0, rows)
+                            both = jnp.dot(one_hot[at, :near], table_hl[:near, :], preferred_element_type=jnp.float32)
+                            near_gap[at, :] = both[:, :LANES] + both[:, LANES:]
+
+            def add_means():
+                with scope("arr_mean%d" % it):
+                    arrive(means.at[it, 1:], flag("means", it, 1))
+
+                with scope("addmean%d" % it):
+                    @pl.loop(0, pairs)
+                    def _(i):
+                        for par in range(2):
+                            for t in range(tiles):
+                                at = rows_of(2 * i + par, t * LANES, LANES)
+                                util[at, :] = util[at, :] + columns(means[it, 2 * i + par, t:t + 1, :])
+
+            def hand_gap():
+                with scope("arr_gapy%d" % it):
+                    arrive(gap.at[it, half], flag("gap", it, 2))
                 for j in range(1, half):
-                    split_into(j, gap[it, j])
-
-            with scope("gnear%d" % it):
-                @pl.loop(0, pairs)
-                def _(i):
-                    for par in range(2):
-                        at = rows_of(2 * i + par, 0, rows)
-                        both = jnp.dot(one_hot[at, :near], table_hl[:near, :], preferred_element_type=jnp.float32)
-                        near_gap[at, :] = both[:, :LANES] + both[:, LANES:]
-
-            with scope("arr_mean%d" % it):
-                arrive(means.at[it, 1:], flag("means", it, 1))
-
-            with scope("addmean%d" % it):
-                @pl.loop(0, pairs)
-                def _(i):
-                    for par in range(2):
-                        for t in range(tiles):
-                            at = rows_of(2 * i + par, t * LANES, LANES)
-                            util[at, :] = util[at, :] + columns(means[it, 2 * i + par, t:t + 1, :])
+                    send(
+                        gap.at[it, half], gap.at[it, half + j], flag("gap", it, 0), flag("gap", it, 3), market_device(j)
+                    )
+
+            add_near()
+            hand_gap()
+            add_means()
 
             with scope("arr_gap%d" % it):
-                arrive(gap.at[it, half:], flag("gap", it, 2))
+                arrive(gap.at[it, half + 1:], flag("gap", it, 3))
                 for j in range(half, groups):
                     split_into(j, gap[it, j])
 

time: 64 us -> 63.1 us (0.986)
  Pallas kernels: 62 us -> 61.1 us
    pallas_call x1, Pallas kernels: 62 us -> 61.1 us  [local(): pl.pallas_call(functools.partial(kernel, dims), out_shape=(pltpu.VMEM((n_...]
where the time goes in v4:
time: 63.1 us; the launch traced here: 63 us
  Pallas kernels  61.1 us (97%)
  local copies, waits for them, and re-layouts  1.23 us (2%)
  between operations  0.64 us (1%)
    pallas_call x1, Pallas kernels, local(): pl.pallas_call(functools.partial(kernel, dims), out_shape=(pltpu.VMEM((n_...  61.1 us

profile of v4, /device:TPU:0, one launch (start us, length us, event | category | flops | bytes accessed | tf_op | source)
XLA Modules:
  0.0 63.0 jit_solution(15891900198291511556)
XLA Ops:
  0.6 61.1 %shard_map.122 = (f32[16,64]{1,0:T(8,128)S(1)}, f32[16,1024]{1,0:T(8,128)S(1)}) custom-call(f32[16]{0:T(128)} %size_h.1, f32[5]{0:T(128)} %scale_h.1, f32[80,1024]{1,0:T(8,128)} %bitcast.5, f32[16,1024]{1,0:T(8,128)} %weight_h.1, f32[5,16,64]{2,1,0:T(8,128)} %bitcast.6, s32[16,64]{1,0:T(8,128)} %firm_h.1, f32[16,64]{1,0:T(8,128)} %mean_h.1, ...), custom_call_target="tpu_custom_call" | custom-call | tf_op jit(solution)/shard_map/pallas_call | solution.py:627
  61.7 0.6 copy.15
  62.3 0.6 copy.16

commit v5 on v4

--- a/solution.py
+++ b/solution.py
@@ -111,10 +111,10 @@
 
     barrier = pltpu.get_barrier_semaphore()
 
-    @pl.loop(1, n)
-    def _(d):
-        t = (me + d) % n
-        pl.semaphore_signal(barrier, inc=1, device_id=(t // grp, t % grp), device_id_type=MESH)
+    for d in range(1, rb):
+        pl.semaphore_signal(barrier, inc=1, device_id=type_device(d), device_id_type=MESH)
+    for j in range(1, groups):
+        pl.semaphore_signal(barrier, inc=1, device_id=market_device(j), device_id_type=MESH)
 
     for key in ("weight", "traits", "firm", "mean", "size", "scale"):
         inputs[key].wait()
@@ -127,7 +127,7 @@
         mass_own[m:m + 1, :] = weight_ref[m:m + 1, :] * size_ref[m]
 
     with scope("bar"):
-        pl.semaphore_wait(barrier, n - 1)
+        pl.semaphore_wait(barrier, rb + groups - 2)
 
     for d in range(1, rb):
         send(loy_h.at[:, lanes_of(type_lane(d))], loy.at[d], flag("loy", 0), flag("loy", 1), type_device(d))

time: 63.1 us -> 62.7 us (level)
  no operation moved by 1% of the time
where the time goes in v5:
time: 62.7 us; the launch traced here: 62.6 us
  Pallas kernels  60.7 us (97%)
  local copies, waits for them, and re-layouts  1.23 us (2%)
  between operations  0.64 us (1%)
    pallas_call x1, Pallas kernels, local(): pl.pallas_call(functools.partial(kernel, dims), out_shape=(pltpu.VMEM((n_...  60.7 us

profile of v5, /device:TPU:0, one launch (start us, length us, event | category | flops | bytes accessed | tf_op | source)
XLA Modules:
  0.0 62.6 jit_solution(8637372430094102836)
XLA Ops:
  0.6 60.7 %shard_map.122 = (f32[16,64]{1,0:T(8,128)S(1)}, f32[16,1024]{1,0:T(8,128)S(1)}) custom-call(f32[16]{0:T(128)} %size_h.1, f32[5]{0:T(128)} %scale_h.1, f32[80,1024]{1,0:T(8,128)} %bitcast.5, f32[16,1024]{1,0:T(8,128)} %weight_h.1, f32[5,16,64]{2,1,0:T(8,128)} %bitcast.6, s32[16,64]{1,0:T(8,128)} %firm_h.1, f32[16,64]{1,0:T(8,128)} %mean_h.1, ...), custom_call_target="tpu_custom_call" | custom-call | tf_op jit(solution)/shard_map/pallas_call | solution.py:627
  61.4 0.6 copy.15
  62.0 0.6 %copy.16 = f32[16,1024]{1,0:T(8,128)} copy(f32[16,1024]{1,0:T(8,128)S(1)} %get-tuple-element.3) | data formatting | bytes 131072
